TPU v7x, 32 devices: a whole 2x2x4 slice. The times are simulated.
32 devices in a mesh: row: 4 (over z), col: 8 (over y, x, core).
Axes of the slice: x: 2, y: 2, z: 4, core: 2. Of those that a mesh axis runs over, the one named last changes fastest.
Arguments:
- fine_residual: bfloat16 [16, 524288], P(None, ('row', 'col')), may hold values from -6 to 6
- tiles_one: bfloat16 [8192, 128, 128], P(('row', 'col')), may hold values from -0.1875 to 0.1875
- pointers_one: int32 [4128], P(('row', 'col')), may hold values from 0 to 256, as said below
- columns_one: int32 [8192], P(('row', 'col')), may hold values from 0 to 1023, as said below
- points_one: int32 [131072], P(('col', 'row')), may hold values from 0 to 16383, as said below
- tiles_two: bfloat16 [4096, 128, 128], P(('row', 'col')), may hold values from -0.125 to 0.125
- pointers_two: int32 [2080], P(('row', 'col')), may hold values from 0 to 128, as said below
- columns_two: int32 [4096], P(('row', 'col')), may hold values from 0 to 127
- points_two: int32 [32768], P(('row', 'col')), may hold values from 0 to 4095, as said below
- tiles_three: bfloat16 [512, 128, 128], P(('row', 'col')), may hold values from -0.1875 to 0.1875
- pointers_three: int32 [288], P(('row', 'col')), may hold values from 0 to 16, as said below
- columns_three: int32 [512], P(('row', 'col')), may hold values from 0 to 63
- points_three: int32 [8192], P(('col', 'row')), may hold values from 0 to 1023, as said below
Outputs:
- coarse_one: bfloat16 [16, 131072], P(None, ('col', 'row'))
- coarse_two: bfloat16 [16, 32768], P(None, ('row', 'col'))
- coarse_three: bfloat16 [16, 8192], P(None, ('col', 'row'))
Inputs may be any that keep to these rules, and one draw needn't show every extreme that they name: `pointers_one`: each tile set's 128 + 1 pointers start at 0 and never fall; the last is that set's live slot count, at most 256; some set has 256 live slots. `pointers_two`: each tile set's 64 + 1 pointers start at 0 and never fall; the last is that set's live slot count, at most 128; some set has 128 live slots. `pointers_three`: each tile set's 8 + 1 pointers start at 0 and never fall; the last is that set's live slot count, at most 16; some set has 16 live slots. `columns_one`: among the live slots of one tile set, at most 32 name block columns with the same quotient by 128; some set reaches 32. `points_one`: values are distinct within each aligned run of 4096 entries. `points_two`: values are distinct within each aligned run of 1024 entries. `points_three`: values are distinct within each aligned run of 256 entries.
All inputs are finite; a program needn't handle non-finite values.
Results may differ from a plain program's by a relative error of at most 0.0057.
Values may be sent and summed in bfloat16 or wider, within the bound.
A program may use at most 128 MiB of HBM per device.

v0:
```python
import functools

import jax
import jax.numpy as jnp
from jax import lax
from jax.experimental import pallas as pl
from jax.experimental.pallas import tpu as pltpu
from jax.sharding import PartitionSpec as P


def split_blocks(piece, edge):
    vectors = piece.shape[0]
    return jnp.transpose(piece.reshape(vectors, piece.shape[1] // edge, edge), (1, 0, 2))


def join_blocks(blocks):
    return jnp.transpose(blocks, (1, 0, 2)).reshape(blocks.shape[1], blocks.shape[0] * blocks.shape[2])


def restrict_kernel(step_slots, batch, index_ref, segment_ref, tiles_ref, source_ref, out_ref, total):
    step = pl.program_id(0)
    blocks, vectors, edge = out_ref.shape

    @pl.when(step == 0)
    def _():
        total[...] = jnp.zeros_like(total)

    def some(part, carry):
        first = part * batch
        products = []
        for i in range(0, batch, 2):
            slot = step * step_slots + first + i
            pair = jnp.concatenate([source_ref[index_ref[slot]], source_ref[index_ref[slot + 1]]], axis=0)
            both = lax.dot_general(
                pair,
                tiles_ref[pl.ds(first + i, 2)].reshape(2 * edge, edge),
                (((1,), (1,)), ((), ())),
                preferred_element_type=jnp.float32,
            )
            products.append(both[:vectors, :edge])
            products.append(both[vectors:, edge:])
        for i in range(batch):
            row = segment_ref[step * step_slots + first + i]
            total[row] = total[row] + products[i]
        return carry

    lax.fori_loop(0, step_slots // batch, some, 0)

    @pl.when(step == pl.num_programs(0) - 1)
    def _():
        out_ref[...] = total[:blocks].astype(out_ref.dtype)


def restrict(tiles, source, index, segment, blocks):
    slots, edge, _ = tiles.shape
    vectors = source.shape[1]
    step_slots = min(slots, 64)
    batch = min(step_slots, 8)
    return pl.pallas_call(
        functools.partial(restrict_kernel, step_slots, batch),
        grid_spec=pltpu.PrefetchScalarGridSpec(
            num_scalar_prefetch=2,
            grid=(slots // step_slots,),
            in_specs=[
                pl.BlockSpec((step_slots, edge, edge), lambda s, a, b: (s, 0, 0)),
                pl.BlockSpec(memory_space=pltpu.VMEM),
            ],
            out_specs=pl.BlockSpec(memory_space=pltpu.VMEM),
            scratch_shapes=[pltpu.VMEM((blocks + 1, vectors, edge), jnp.float32)],
        ),
        out_shape=jax.ShapeDtypeStruct((blocks, vectors, edge), jnp.bfloat16),
        cost_estimate=pl.CostEstimate(
            flops=2 * slots * vectors * edge * edge, bytes_accessed=2 * tiles.size, transcendentals=0
        ),
        name="restrict",
    )(index, segment, tiles, source)


def points_kernel(group, span, points_ref, source_ref, out_ref):
    chunks, vectors, edge = out_ref.shape
    blocks = source_ref.shape[0]

    def one_group(number, carry):
        points = points_ref[number]
        owners = jnp.broadcast_to(points // edge, (vectors, group * edge))
        lanes = jnp.broadcast_to(points % edge, (edge, group * edge))
        spots = lax.broadcasted_iota(jnp.int32, (edge, group * edge), 0)
        pick = (lanes == spots).astype(jnp.float32).astype(jnp.bfloat16)
        found = jnp.zeros((vectors, group * edge), jnp.float32)
        for part in range(blocks // span):
            rows = source_ref[part * span : (part + 1) * span].reshape(span * vectors, edge)
            moved = jnp.dot(rows, pick, preferred_element_type=jnp.float32)
            for k in range(span):
                here = moved[k * vectors : (k + 1) * vectors]
                found = jnp.where(owners == part * span + k, here, found)
        for i in range(group):
            out_ref[number * group + i] = found[:, i * edge : (i + 1) * edge].astype(out_ref.dtype)
        return carry

    lax.fori_loop(0, chunks // group, one_group, 0)


def pick_points(points, source):
    blocks, vectors, edge = source.shape
    chunks = points.shape[0] // edge
    group = min(chunks, 2)
    return pl.pallas_call(
        functools.partial(points_kernel, group, min(blocks, 32)),
        in_specs=[pl.BlockSpec(memory_space=pltpu.VMEM)] * 2,
        out_specs=pl.BlockSpec(memory_space=pltpu.VMEM),
        out_shape=jax.ShapeDtypeStruct((chunks, vectors, edge), source.dtype),
        cost_estimate=pl.CostEstimate(
            flops=8 * chunks * blocks * vectors * edge, bytes_accessed=source.size * 2, transcendentals=0
        ),
        name="points",
    )(points.reshape(chunks // group, 1, group * edge), source)


def segments(pointers, slots):
    positions = jnp.arange(slots, dtype=jnp.int32)
    return jnp.sum((pointers[None, :] <= positions[:, None]).astype(jnp.int32), axis=1) - 1


def exchange_kernel(axis, peers, gather, partial_ref, injected_ref, *rest):
    if gather:
        own_ref, group_ref, arrived, sent, landed, sent_own, landed_own = rest
    else:
        own_ref, arrived, sent, landed = rest
    me = lax.axis_index(axis)
    others = [lax.rem(me + k, peers) for k in range(1, peers)]
    barrier = pltpu.get_barrier_semaphore()
    for peer in others:
        pl.semaphore_signal(barrier, inc=1, device_id={axis: peer}, device_id_type=pl.DeviceIdType.MESH)
    pl.semaphore_wait(barrier, peers - 1)

    chunks = sent.shape[0]
    size = injected_ref.shape[0] // chunks
    parts = [pl.ds(h * size, size) for h in range(chunks)]

    def copies(source, target, out_sem, in_sem, h):
        started = []
        for k, peer in enumerate(others):
            copy = pltpu.make_async_remote_copy(
                src_ref=source(peer),
                dst_ref=target(k),
                send_sem=out_sem.at[h, k],
                recv_sem=in_sem.at[h, k],
                device_id={axis: peer},
                device_id_type=pl.DeviceIdType.MESH,
            )
            copy.start()
            started.append(copy)
        return started

    first, again = [], []
    for h, part in enumerate(parts):
        first.append(
            copies(lambda peer: partial_ref.at[peer, part], lambda k: arrived.at[k, part], sent, landed, h)
        )
    for h, part in enumerate(parts):
        total = partial_ref[me, part].astype(jnp.float32) + injected_ref[part].astype(jnp.float32)
        for k, copy in enumerate(first[h]):
            copy.wait_recv()
            total = total + arrived[k, part].astype(jnp.float32)
        own_ref[part] = total.astype(own_ref.dtype)
        if gather:
            again += copies(
                lambda peer: own_ref.at[part], lambda k: group_ref.at[me, part], sent_own, landed_own, h
            )
            group_ref[me, part] = total.astype(own_ref.dtype)
    for started in first:
        for copy in started:
            copy.wait_send()
    for copy in again:
        copy.wait()


def own_sum(partial, injected, axis, number, gather):
    peers = lax.axis_size(axis)
    piece = (partial.shape[0] // peers,) + partial.shape[1:]
    pieces = partial.reshape((peers,) + piece)
    kind = partial.dtype
    chunks = 2 if piece[0] % 32 == 0 else 1
    shapes = [jax.ShapeDtypeStruct(piece, kind)]
    scratch = [pltpu.VMEM((peers - 1,) + piece, kind)] + [pltpu.SemaphoreType.DMA((chunks, peers - 1))] * 2
    if gather:
        shapes.append(jax.ShapeDtypeStruct((peers,) + piece, kind))
        scratch += [pltpu.SemaphoreType.DMA((chunks, peers - 1))] * 2
    found = pl.pallas_call(
        functools.partial(exchange_kernel, axis, peers, gather),
        in_specs=[pl.BlockSpec(memory_space=pltpu.VMEM)] * 2,
        out_specs=[pl.BlockSpec(memory_space=pltpu.VMEM)] * len(shapes),
        out_shape=shapes,
        scratch_shapes=scratch,
        compiler_params=pltpu.CompilerParams(collective_id=number, has_side_effects=True),
        name="exchange",
    )(pieces, injected)
    if gather:
        return found[0], found[1].reshape(partial.shape)
    return found[0]


def on_device(
    fine_residual,
    tiles_one,
    pointers_one,
    columns_one,
    points_one,
    tiles_two,
    pointers_two,
    columns_two,
    points_two,
    tiles_three,
    pointers_three,
    columns_three,
    points_three,
):
    edge = tiles_one.shape[1]
    slots = tiles_one.shape[0]
    blocks_one = pointers_one.shape[0] - 1
    peers = lax.axis_size("col")
    per_peer = slots // peers
    blocks_peer = fine_residual.shape[1] // edge
    positions = jnp.arange(slots, dtype=jnp.int32)
    segment_one = segments(pointers_one, slots)
    live = segment_one < blocks_one
    owner = columns_one // blocks_peer
    within = columns_one % blocks_peer
    same = (owner[:, None] == owner[None, :]) & (positions[None, :] < positions[:, None])
    rank = jnp.sum(same.astype(jnp.int32), axis=1)
    target = jnp.where(live, owner * per_peer + rank, slots)
    hits = target[None, :] == positions[:, None]
    requests = jnp.sum(jnp.where(hits, within[None, :], 0), axis=1).reshape(peers, per_peer)
    asked = lax.all_to_all(requests, "col", split_axis=0, concat_axis=0, tiled=True)
    own_blocks = split_blocks(fine_residual, edge)
    found = jnp.take(own_blocks, asked.reshape(-1), axis=0, mode="clip")
    found = found.reshape((peers, per_peer) + found.shape[1:])
    replies = lax.all_to_all(found, "col", split_axis=0, concat_axis=0, tiled=True)
    replies = replies.reshape((slots,) + replies.shape[2:])
    injected = pick_points(points_one, own_blocks)
    partial = restrict(
        tiles_one, replies, jnp.minimum(target, slots - 1), segment_one, blocks_one
    )
    coarse_one, group = own_sum(partial, injected, "row", 0, True)
    injected = pick_points(points_two, coarse_one)
    partial = restrict(
        tiles_two, group, columns_two, segments(pointers_two, tiles_two.shape[0]), pointers_two.shape[0] - 1
    )
    coarse_two, group = own_sum(partial, injected, "col", 1, True)
    injected = pick_points(points_three, coarse_two)
    partial = restrict(
        tiles_three,
        group,
        columns_three,
        segments(pointers_three, tiles_three.shape[0]),
        pointers_three.shape[0] - 1,
    )
    coarse_three = own_sum(partial, injected, "row", 2, False)
    return (join_blocks(coarse_one), join_blocks(coarse_two), join_blocks(coarse_three))


def solution(mesh):
    placed = (
        P(None, ("row", "col")),
        P(("row", "col"), None, None),
        P(("row", "col")),
        P(("row", "col")),
        P(("col", "row")),
        P(("row", "col"), None, None),
        P(("row", "col")),
        P(("row", "col")),
        P(("row", "col")),
        P(("row", "col"), None, None),
        P(("row", "col")),
        P(("row", "col")),
        P(("col", "row")),
    )
    return jax.shard_map(
        on_device,
        mesh=mesh,
        in_specs=placed,
        out_specs=(P(None, ("col", "row")), P(None, ("row", "col")), P(None, ("col", "row"))),
        check_vma=False,
    )
```

profile of v0, /device:TPU:0, one launch (start us, length us, event | category | flops | bytes accessed | tf_op | source)
XLA Modules:
  0.0 112.3 jit_solution(7224143364262265966)
XLA Ops:
  0.6 0.0 copy-start
  0.6 0.8 convert_reduce_fusion.1
  1.5 0.7 and_select_fusion
  2.2 0.2 convert_reduce_fusion
  2.4 0.6 broadcast_minimum_fusion
  2.9 0.1 select_reduce_fusion
  3.1 0.7 all_to_all.9
  3.7 5.2 %all-to-all-start = ((s32[8,1,32]{2,1,0:T(1,128)}), s32[8,1,32]{2,1,0:T(1,128)S(1)}, u32[]{:S(2)}, u32[]{:S(2)}) async-start(s32[8,1,32]{2,1,0:T(1,128)} %all_to_all.9), calls=%async_computation | async-start | bytes 8192 | tf_op jit(solution)/shard_map/all_to_all | solution.py:234
  8.9 0.0 copy-done
  8.9 0.1 bitcast_bitcast_fusion.source_ref
  9.0 0.0 copy-start.1
  9.1 4.5 %all-to-all-done = s32[8,1,32]{2,1,0:T(1,128)S(1)} async-done(((s32[8,1,32]{2,1,0:T(1,128)}), s32[8,1,32]{2,1,0:T(1,128)S(1)}, u32[]{:S(2)}, u32[]{:S(2)}) %all-to-all-start) | async-done | bytes 1056 | tf_op jit(solution)/shard_map/all_to_all | solution.py:234
  13.5 0.5 broadcast.66
  14.1 0.7 reduce.3
  14.7 0.1 reshape.78
  14.8 1.8 %gather_fusion = bf16[256,16,128]{2,1,0:T(8,128)(2,1)} fusion(bf16[128,16,128]{2,1,0:T(8,128)(2,1)S(1)} %bitcast_bitcast_fusion.source_ref, s32[1024]{0:T(1024)S(1)} %pad_clamp_fusion), kind=kCustom, calls=%fused_computation | custom fusion | bytes 2098176 | tf_op jit(solution)/shard_map/jit(_take)/gather | solution.py:236
  16.6 3.6 %all-to-all-start.1 = ((bf16[8,32,16,128]{3,2,1,0:T(8,128)(2,1)}), bf16[8,32,16,128]{3,2,1,0:T(8,128)(2,1)S(1)}, u32[]{:S(2)}, u32[]{:S(2)}) async-start(bf16[8,32,16,128]{3,2,1,0:T(8,128)(2,1)} %bitcast.1), calls=%async_computation.1 | async-start | bytes 2097152 | tf_op jit(solution)/shard_map/all_to_all | solution.py:238
  20.1 0.0 copy-done.1
  20.2 9.1 %points.3.injected_ref = bf16[32,16,128]{2,1,0:T(8,128)(2,1)} custom-call(s32[16,1,256]{2,1,0:T(1,128)} %bitcast.41, bf16[128,16,128]{2,1,0:T(8,128)(2,1)} %copy-done.1), custom_call_target="tpu_custom_call" | custom-call | flops 67108864 | bytes 524288 | tf_op jit(solution)/shard_map/points/pallas_call | solution.py:107
  29.3 0.8 convert_reduce_fusion.3
  30.1 0.7 convert_reduce_fusion.2
  30.8 0.5 broadcast_add_fusion.2.segment_ref
  31.3 0.6 broadcast_add_fusion.1.segment_ref
  31.9 3.6 %all-to-all-done.1 = bf16[8,32,16,128]{3,2,1,0:T(8,128)(2,1)S(1)} async-done(((bf16[8,32,16,128]{3,2,1,0:T(8,128)(2,1)}), bf16[8,32,16,128]{3,2,1,0:T(8,128)(2,1)S(1)}, u32[]{:S(2)}, u32[]{:S(2)}) %all-to-all-start.1) | async-done | bytes 1048608 | tf_op jit(solution)/shard_map/all_to_all | solution.py:238
  35.5 0.0 copy-start.2
  35.5 1.0 copy-done.2
  36.5 10.4 %restrict.3 = bf16[128,16,128]{2,1,0:T(8,128)(2,1)} custom-call(s32[256]{0:T(256)} %get-tuple-element.11.index_ref, s32[256]{0:T(256)} %get-tuple-element.15.segment_ref, bf16[256,128,128]{2,1,0:T(8,128)(2,1)} %tiles_ref.3, bf16[256,16,128]{2,1,0:T(8,128)(2,1)} %bitcast.35), custom_call_target="tpu_custom_call" | custom-call | flops 134217728 | bytes 8388608 | tf_op jit(solution)/shard_map/restrict/pallas_call | solution.py:59
  46.9 25.7 %exchange.3 = (bf16[32,16,128]{2,1,0:T(8,128)(2,1)}, bf16[4,32,16,128]{3,2,1,0:T(8,128)(2,1)}) custom-call(bf16[4,32,16,128]{3,2,1,0:T(8,128)(2,1)} %bitcast.36, bf16[32,16,128]{2,1,0:T(8,128)(2,1)} %points.3.injected_ref), custom_call_target="tpu_custom_call" | custom-call | tf_op jit(solution)/shard_map/exchange/pallas_call | solution.py:189
  72.6 1.6 %copy_bitcast_fusion = bf16[16,4096]{1,0:T(8,128)(2,1)} fusion(bf16[32,16,128]{2,1,0:T(8,128)(2,1)} %get-tuple-element.7.source_ref), kind=kLoop, calls=%fused_computation.9 | loop fusion | bytes 262144 | tf_op jit(solution)/shard_map/reshape | solution.py:17
  74.2 2.5 %points.4.injected_ref = bf16[8,16,128]{2,1,0:T(8,128)(2,1)} custom-call(s32[4,1,256]{2,1,0:T(1,128)} %bitcast.42, bf16[32,16,128]{2,1,0:T(8,128)(2,1)} %get-tuple-element.7.source_ref), custom_call_target="tpu_custom_call" | custom-call | flops 4194304 | bytes 131072 | tf_op jit(solution)/shard_map/points/pallas_call | solution.py:107
  76.7 6.5 %restrict.4 = bf16[64,16,128]{2,1,0:T(8,128)(2,1)} custom-call(s32[128]{0:T(128)} %index_ref.2, s32[128]{0:T(128)} %broadcast_add_fusion.2.segment_ref, bf16[128,128,128]{2,1,0:T(8,128)(2,1)} %tiles_ref.4, bf16[128,16,128]{2,1,0:T(8,128)(2,1)} %bitcast.38), custom_call_target="tpu_custom_call" | custom-call | flops 67108864 | bytes 4194304 | tf_op jit(solution)/shard_map/restrict/pallas_call | solution.py:59
  83.2 15.1 %exchange.4 = (bf16[8,16,128]{2,1,0:T(8,128)(2,1)}, bf16[8,8,16,128]{3,2,1,0:T(8,128)(2,1)}) custom-call(bf16[8,8,16,128]{3,2,1,0:T(8,128)(2,1)} %bitcast.37, bf16[8,16,128]{2,1,0:T(8,128)(2,1)} %points.4.injected_ref), custom_call_target="tpu_custom_call" | custom-call | tf_op jit(solution)/shard_map/exchange/pallas_call | solution.py:189
  98.3 1.4 %copy_bitcast_fusion.1 = bf16[16,1024]{1,0:T(8,128)(2,1)} fusion(bf16[8,16,128]{2,1,0:T(8,128)(2,1)} %get-tuple-element.9.source_ref), kind=kLoop, calls=%fused_computation.12 | loop fusion | bytes 65536 | tf_op jit(solution)/shard_map/reshape | solution.py:17
  99.7 1.5 %points.5.injected_ref = bf16[2,16,128]{2,1,0:T(8,128)(2,1)} custom-call(s32[1,1,256]{2,1,0:T(1,128)} %bitcast.43, bf16[8,16,128]{2,1,0:T(8,128)(2,1)} %get-tuple-element.9.source_ref), custom_call_target="tpu_custom_call" | custom-call | flops 262144 | bytes 32768 | tf_op jit(solution)/shard_map/points/pallas_call | solution.py:107
  101.2 2.8 %restrict.5 = bf16[8,16,128]{2,1,0:T(8,128)(2,1)} custom-call(s32[16]{0:T(128)} %index_ref.3, s32[16]{0:T(128)} %broadcast_add_fusion.1.segment_ref, bf16[16,128,128]{2,1,0:T(8,128)(2,1)} %tiles_ref.5, bf16[64,16,128]{2,1,0:T(8,128)(2,1)} %bitcast.39), custom_call_target="tpu_custom_call" | custom-call | flops 8388608 | bytes 524288 | tf_op jit(solution)/shard_map/restrict/pallas_call | solution.py:59
  104.0 6.9 %exchange.5 = bf16[2,16,128]{2,1,0:T(8,128)(2,1)} custom-call(bf16[4,2,16,128]{3,2,1,0:T(8,128)(2,1)} %bitcast.40, bf16[2,16,128]{2,1,0:T(8,128)(2,1)} %points.5.injected_ref), custom_call_target="tpu_custom_call" | custom-call | tf_op jit(solution)/shard_map/exchange/pallas_call | solution.py:189
  111.0 1.3 %copy_bitcast_fusion.2 = bf16[16,256]{1,0:T(8,128)(2,1)} fusion(bf16[2,16,128]{2,1,0:T(8,128)(2,1)} %exchange.5), kind=kLoop, calls=%fused_computation.13 | loop fusion | bytes 16384 | tf_op jit(solution)/shard_map/reshape | solution.py:17
  (1 shorter events, 0.0 us)
Async XLA Ops:
  0.6 8.3 %copy-start = (bf16[16,16384]{1,0:T(8,128)(2,1)S(1)}, bf16[16,16384]{1,0:T(8,128)(2,1)}, u32[]{:S(2)}) copy-start(bf16[16,16384]{1,0:T(8,128)(2,1)} %param.13) | copy-start | bytes 1572868
  3.7 9.8 %all-to-all-start = ((s32[8,1,32]{2,1,0:T(1,128)}), s32[8,1,32]{2,1,0:T(1,128)S(1)}, u32[]{:S(2)}, u32[]{:S(2)}) async-start(s32[8,1,32]{2,1,0:T(1,128)} %all_to_all.9), calls=%async_computation | async-start | bytes 8192 | tf_op jit(solution)/shard_map/all_to_all | solution.py:234
  9.0 11.1 %copy-start.1 = (bf16[128,16,128]{2,1,0:T(8,128)(2,1)}, bf16[128,16,128]{2,1,0:T(8,128)(2,1)S(1)}, u32[]{:S(2)}) copy-start(bf16[128,16,128]{2,1,0:T(8,128)(2,1)S(1)} %bitcast_bitcast_fusion.source_ref) | copy-start | bytes 1572868
  16.6 18.9 %all-to-all-start.1 = ((bf16[8,32,16,128]{3,2,1,0:T(8,128)(2,1)}), bf16[8,32,16,128]{3,2,1,0:T(8,128)(2,1)S(1)}, u32[]{:S(2)}, u32[]{:S(2)}) async-start(bf16[8,32,16,128]{3,2,1,0:T(8,128)(2,1)} %bitcast.1), calls=%async_computation.1 | async-start | bytes 2097152 | tf_op jit(solution)/shard_map/all_to_all | solution.py:238
  35.5 1.0 copy-start.2
where the time goes:
time: 113 us; the launch traced here: 112 us
  Pallas kernels  80.7 us (71%)
  starting transfers between devices  8.76 us (8%)
  local copies, waits for them, and re-layouts  8.38 us (7%)
  waiting for transfers between devices  8.05 us (7%)
  other arithmetic  5.69 us (5%)
    pallas_call x3, Pallas kernels, own_sum(): pl.pallas_call(functools.partial(exchange_kernel, axis, peers, gather), i...  47.8 us
    pallas_call x3, Pallas kernels, restrict(): pl.pallas_call(functools.partial(restrict_kernel, step_slots, batch), gri...  19.7 us
    pallas_call x3, Pallas kernels, pick_points(): pl.pallas_call(functools.partial(points_kernel, group, min(blocks, 32)),...  13.1 us
    all_to_all x1, starting transfers between devices, on_device(): lax.all_to_all(requests, 'col', split_axis=0, concat_axis=0, tiled=True)  5.2 us
    all_to_all x1, waiting for transfers between devices, on_device(): lax.all_to_all(requests, 'col', split_axis=0, concat_axis=0, tiled=True)  4.5 us
    reshape x3, local copies, waits for them, and re-layouts, join_blocks(): jnp.transpose(blocks, (1, 0, 2))  4.24 us
    all_to_all x1, starting transfers between devices, on_device(): lax.all_to_all(found, 'col', split_axis=0, concat_axis=0, tiled=True)  3.56 us
    all_to_all x1, waiting for transfers between devices, on_device(): lax.all_to_all(found, 'col', split_axis=0, concat_axis=0, tiled=True)  3.55 us
  transfers between devices with their start and end apart: 2, of which 2 were waited for; matrix products, arithmetic and copies ran while one was open for 2% of the time, Pallas kernels for 8%

commit v1 on v0

v1 whole, which is shorter than its diff:
```python
import functools

import jax
import jax.numpy as jnp
from jax import lax
from jax.experimental import pallas as pl
from jax.experimental.pallas import tpu as pltpu
from jax.sharding import PartitionSpec as P

CHUNKS = 2
BATCH = 16


def mirrored(index, mask, count):
    flipped = index
    bit = 1
    while bit < count:
        if mask & bit:
            flipped = flipped + bit * (1 - 2 * lax.rem(index // bit, 2))
        bit *= 2
    return flipped


def mirror_order(count):
    return sorted(range(1, count), key=lambda mask: (bin(mask).count("1"), mask))


def shift_of(size):
    assert size & (size - 1) == 0
    return size.bit_length() - 1


def down(row):
    edge = 128
    parts = []
    for first in range(0, row.shape[1], edge):
        spread = jnp.broadcast_to(row[:, first : first + edge], (edge, edge))
        parts.append(jnp.transpose(spread, (1, 0)))
    return parts


def plan(columns_ref, live, peers, blocks_peer, requests_ref, slots_ref, targets_ref):
    slots = columns_ref.shape[1]
    edge = 128
    per_peer = slots // peers
    columns = columns_ref[...]
    places = lax.broadcasted_iota(jnp.int32, (1, slots), 1)
    owner = jnp.right_shift(columns, shift_of(blocks_peer))
    within = jnp.bitwise_and(columns, blocks_peer - 1)
    owner = jnp.where(places < live, owner, peers + places)
    rank = jnp.zeros((1, slots), jnp.int32)
    owners_down = down(owner)
    for part, other in enumerate(owners_down):
        lines = lax.broadcasted_iota(jnp.int32, (edge, edge), 0) + part * edge
        ranks = []
        for first in range(0, slots, edge):
            lanes = lax.broadcasted_iota(jnp.int32, (edge, edge), 1) + first
            here = jnp.broadcast_to(owner[:, first : first + edge], (edge, edge))
            same = jnp.where((other == here) & (lines < lanes), 1, 0)
            ranks.append(jnp.sum(same, axis=0, keepdims=True))
        rank = rank + jnp.concatenate(ranks, axis=1)
    target = jnp.where(places < live, owner * per_peer + rank, slots)
    targets_ref[...] = jnp.where(places < live, target, 0)
    targets_down = down(target)
    within_down = down(within)
    for first in range(0, slots, edge):
        lanes = lax.broadcasted_iota(jnp.int32, (edge, edge), 1) + first
        request = jnp.zeros((1, edge), jnp.int32)
        slot = jnp.zeros((1, edge), jnp.int32)
        for part in range(slots // edge):
            lines = lax.broadcasted_iota(jnp.int32, (edge, edge), 0) + part * edge
            hit = targets_down[part] == lanes
            request = request + jnp.sum(jnp.where(hit, within_down[part], 0), axis=0, keepdims=True)
            slot = slot + jnp.sum(jnp.where(hit, lines, 0), axis=0, keepdims=True)
        requests_ref[:, first : first + edge] = request
        slots_ref[:, first : first + edge] = slot


def pair_products(tiles, sources):
    none = jnp.zeros_like(sources[0])
    left = jnp.concatenate([sources[0], none], axis=1)
    right = jnp.concatenate([none, sources[1]], axis=1)
    both = lax.dot_general(
        jnp.concatenate([left, right], axis=0),
        jnp.concatenate(tiles, axis=1),
        (((1,), (1,)), ((), ())),
        preferred_element_type=jnp.float32,
    )
    vectors = sources[0].shape[0]
    return both[:vectors], both[vectors:]


def some_products(tiles_ref, number, tile_of, source_of):
    products = []
    for i in range(0, number, 2):
        products += pair_products(
            [tiles_ref[tile_of(i)], tiles_ref[tile_of(i + 1)]], [source_of(i), source_of(i + 1)]
        )
    return products


def points_groups(first, last, points_ref, block_of, blocks, span, out_ref):
    edge = out_ref.shape[2]
    vectors = out_ref.shape[1]
    wide = points_ref.shape[2]
    group = wide // edge

    def one_group(number, carry):
        points = points_ref[number]
        owners = jnp.broadcast_to(jnp.right_shift(points, shift_of(edge)), (vectors, wide))
        lanes = jnp.broadcast_to(jnp.bitwise_and(points, edge - 1), (edge, wide))
        spots = lax.broadcasted_iota(jnp.int32, (edge, wide), 0)
        pick = (lanes == spots).astype(jnp.float32).astype(jnp.bfloat16)
        found = jnp.zeros((vectors, wide), jnp.float32)
        for part in range(blocks // span):
            rows = jnp.concatenate([block_of(part * span + k) for k in range(span)], axis=0)
            moved = jnp.dot(rows, pick, preferred_element_type=jnp.float32)
            for k in range(span):
                here = moved[k * vectors : (k + 1) * vectors]
                found = jnp.where(owners == part * span + k, here, found)
        for i in range(group):
            out_ref[number * group + i] = found[:, i * edge : (i + 1) * edge]
        return carry

    lax.fori_loop(first, last, one_group, 0)


def kernel(
    axes,
    fine_ref,
    columns_ref,
    tiles_one,
    tiles_two,
    tiles_three,
    pointers_one,
    pointers_two,
    pointers_three,
    columns_two,
    columns_three,
    points_one,
    points_two,
    points_three,
    out_one,
    out_two,
    out_three,
    requests_v,
    slots_v,
    targets_v,
    asked_v,
    slots_s,
    targets_s,
    asked_s,
    fine_blocks,
    replies_out,
    replies,
    held_one,
    held_two,
    held_three,
    products_one,
    sums_one,
    sums_two,
    sums_three,
    partial_one,
    partial_two,
    partial_three,
    arrived_one,
    arrived_two,
    arrived_three,
    injected_one,
    injected_two,
    injected_three,
    group_one,
    group_two,
    local_sem,
    request_sem,
    reply_sem,
    sum_one_sem,
    own_one_sem,
    sum_two_sem,
    own_two_sem,
    sum_three_sem,
):
    rows, cols = axes
    row, col = lax.axis_index("row"), lax.axis_index("col")
    edge = held_one.shape[2]
    slots = columns_ref.shape[1]
    per_peer = slots // cols
    blocks_peer = fine_ref.shape[1] // edge
    row_peers = [(k, lax.rem(row + k, rows)) for k in range(1, rows)]
    col_peers = [(m, mirrored(col, m, cols)) for m in mirror_order(cols)]
    mesh_id = pl.DeviceIdType.MESH

    barrier = pltpu.get_barrier_semaphore()
    for _, peer in row_peers:
        pl.semaphore_signal(barrier, inc=1, device_id={"row": peer}, device_id_type=mesh_id)
    for _, peer in col_peers:
        pl.semaphore_signal(barrier, inc=1, device_id={"col": peer}, device_id_type=mesh_id)
    loads = [
        pltpu.make_async_copy(source, held, local_sem.at[i])
        for i, (source, held) in enumerate(
            [(tiles_one, held_one), (tiles_two, held_two), (tiles_three, held_three)]
        )
    ]
    for load in loads:
        load.start()

    for j in range(blocks_peer):
        fine_blocks[j] = fine_ref[:, j * edge : (j + 1) * edge]
    plan(columns_ref, pointers_one[pointers_one.shape[0] - 1], cols, blocks_peer, requests_v, slots_v, targets_v)
    plans = [
        pltpu.make_async_copy(requests_v, asked_s.at[0], local_sem.at[3]),
        pltpu.make_async_copy(slots_v, slots_s, local_sem.at[4]),
        pltpu.make_async_copy(targets_v, targets_s, local_sem.at[5]),
    ]
    for copy in plans:
        copy.start()
    pl.semaphore_wait(barrier, rows + cols - 2)

    def send(source, target, sems, at, device):
        copy = pltpu.make_async_remote_copy(
            src_ref=source,
            dst_ref=target,
            send_sem=sems.at[(0,) + at],
            recv_sem=sems.at[(1,) + at],
            device_id=device,
            device_id_type=mesh_id,
        )
        copy.start()
        return copy

    asks = [send(requests_v, asked_v.at[m - 1], request_sem, (m - 1,), {"col": peer}) for m, peer in col_peers]
    for copy in plans:
        copy.wait()

    def take(m, out_ref, place):
        base = col * per_peer

        def some(step, carry):
            for i in range(8):
                at = step * 8 + i
                out_ref[place, at] = fine_blocks[asked_s[m, 0, base + at]]
            return carry

        lax.fori_loop(0, per_peer // 8, some, 0)

    def products_of(m, owner):
        base = owner * per_peer
        batch = min(BATCH, per_peer)

        def some(step, carry):
            first = step * batch
            found = some_products(
                held_one,
                batch,
                lambda i: slots_s[0, base + first + i],
                lambda i: replies[m, first + i],
            )
            for i, product in enumerate(found):
                products_one[base + first + i] = product
            return carry

        lax.fori_loop(0, per_peer // batch, some, 0)

    groups = points_one.shape[0]
    span_one = min(blocks_peer, 32)

    def fine_static(j):
        return fine_blocks[j]

    def points_at_one(first, last):
        points_groups(first, last, points_one, fine_static, blocks_peer, span_one, injected_one)

    take(0, replies, 0)
    loads[0].wait()
    products_of(0, col)
    points_at_one(0, groups // 8)
    for copy in asks:
        copy.wait_recv()
    asked = pltpu.make_async_copy(asked_v, asked_s.at[pl.ds(1, cols - 1)], local_sem.at[6])
    asked.start()
    asked.wait()
    answers = []
    for m, peer in col_peers:
        take(m, replies_out, m - 1)
        answers.append(send(replies_out.at[m - 1], replies.at[m], reply_sem, (m - 1,), {"col": peer}))
    points_at_one(groups // 8, groups // 4)
    for (m, peer), copy in zip(col_peers, answers):
        copy.wait_recv()
        products_of(m, peer)

    def run_one(step, total):
        for i in range(8):
            at = step * 8 + i
            total = total + products_one[targets_s[0, at]]
            sums_one[at + 1] = total
        return total

    sums_one[0] = jnp.zeros(sums_one.shape[1:], jnp.float32)
    lax.fori_loop(0, slots // 8, run_one, jnp.zeros(sums_one.shape[1:], jnp.float32))

    def block_sum(sums, pointers, block):
        return sums[pointers[block + 1]] - sums[pointers[block]]

    def partials(sums, pointers, partial, piece, first, size):
        per_piece = partial.shape[1]
        step_size = min(size, 8)

        def some(step, carry):
            for i in range(step_size):
                at = first + step * step_size + i
                partial[piece, at] = block_sum(sums, pointers, piece * per_piece + at).astype(partial.dtype)
            return carry

        lax.fori_loop(0, size // step_size, some, 0)

    def exchange(sums, pointers, partial, arrived, injected, chunks, peers, axis, me, sems, inject, group, own_sems, out):
        size = partial.shape[1] // chunks
        parts = [pl.ds(h * size, size) for h in range(chunks)]
        first, again = [], []
        for h, part in enumerate(parts):
            started = []
            for k, peer in peers:
                partials(sums, pointers, partial, peer, h * size, size)
                started.append(
                    send(partial.at[peer, part], arrived.at[k - 1, part], sems, (h, k - 1), {axis: peer})
                )
            first.append(started)
        inject()
        for h, part in enumerate(parts):
            base = me * partial.shape[1] + h * size
            own = [
                block_sum(sums, pointers, base + i) + injected[h * size + i] for i in range(size)
            ]
            for (k, _), copy in zip(peers, first[h]):
                copy.wait_recv()
                for i in range(size):
                    own[i] = own[i] + arrived[k - 1, h * size + i].astype(jnp.float32)
            for i in range(size):
                value = own[i].astype(out.dtype)
                at = h * size + i
                out[:, at * edge : (at + 1) * edge] = value
                if group is not None:
                    group[me, at] = value
            if group is not None:
                for k, peer in peers:
                    again.append(
                        send(group.at[me, part], group.at[me, part], own_sems, (h, k - 1), {axis: peer})
                    )
        return [copy for started in first for copy in started], again

    def restrict(held, columns, group, sums):
        number = held.shape[0]
        batch = min(BATCH, number)
        per_piece = group.shape[1]

        def some(step, total):
            first = step * batch

            def source_of(i):
                column = columns[first + i]
                return group[jnp.right_shift(column, shift_of(per_piece)), jnp.bitwise_and(column, per_piece - 1)]

            found = some_products(held, batch, lambda i: first + i, source_of)
            for i, product in enumerate(found):
                total = total + product
                sums[first + i + 1] = total
            return total

        sums[0] = jnp.zeros(sums.shape[1:], jnp.float32)
        lax.fori_loop(0, number // batch, some, jnp.zeros(sums.shape[1:], jnp.float32))

    sent_one, own_one = exchange(
        sums_one, pointers_one, partial_one, arrived_one, injected_one, sum_one_sem.shape[1], row_peers, "row", row,
        sum_one_sem, lambda: points_at_one(groups // 4, groups), group_one, own_one_sem, out_one,
    )

    def own_block_one(j):
        return group_one[row, j]

    points_groups(
        0, points_two.shape[0], points_two, own_block_one, group_one.shape[1], min(group_one.shape[1], 32), injected_two
    )
    loads[1].wait()
    for copy in own_one:
        copy.wait_recv()
    restrict(held_two, columns_two, group_one, sums_two)
    sent_two, own_two = exchange(
        sums_two, pointers_two, partial_two, arrived_two, injected_two, sum_two_sem.shape[1], col_peers, "col", col,
        sum_two_sem, lambda: None, group_two, own_two_sem, out_two,
    )

    def own_block_two(j):
        return group_two[col, j]

    points_groups(
        0, points_three.shape[0], points_three, own_block_two, group_two.shape[1], group_two.shape[1], injected_three
    )
    loads[2].wait()
    for copy in own_two:
        copy.wait_recv()
    restrict(held_three, columns_three, group_two, sums_three)
    sent_three, _ = exchange(
        sums_three, pointers_three, partial_three, arrived_three, injected_three, sum_three_sem.shape[1], row_peers,
        "row", row, sum_three_sem, lambda: None, None, None, out_three,
    )
    for copy in asks + answers + sent_one + own_one + sent_two + own_two + sent_three:
        copy.wait_send()


def on_device(
    fine_residual,
    tiles_one,
    pointers_one,
    columns_one,
    points_one,
    tiles_two,
    pointers_two,
    columns_two,
    points_two,
    tiles_three,
    pointers_three,
    columns_three,
    points_three,
):
    vectors = fine_residual.shape[0]
    edge = tiles_one.shape[1]
    rows, cols = lax.axis_size("row"), lax.axis_size("col")
    slots = tiles_one.shape[0]
    per_peer = slots // cols
    low, wide = fine_residual.dtype, jnp.float32
    piece_one = (pointers_one.shape[0] - 1) // rows
    piece_two = (pointers_two.shape[0] - 1) // cols
    piece_three = (pointers_three.shape[0] - 1) // rows
    chunks = CHUNKS if piece_one % CHUNKS == 0 else 1

    def grouped(points):
        size = points.shape[0] // edge
        group = min(size, 2)
        return points.reshape(size // group, 1, group * edge)

    block = (vectors, edge)
    vmem = pl.BlockSpec(memory_space=pltpu.VMEM)
    smem = pl.BlockSpec(memory_space=pltpu.SMEM)
    hbm = pl.BlockSpec(memory_space=pl.ANY)
    dma = pltpu.SemaphoreType.DMA
    scratch = [
        pltpu.VMEM((1, slots), jnp.int32),
        pltpu.VMEM((1, slots), jnp.int32),
        pltpu.VMEM((1, slots), jnp.int32),
        pltpu.VMEM((cols - 1, 1, slots), jnp.int32),
        pltpu.SMEM((1, slots), jnp.int32),
        pltpu.SMEM((1, slots), jnp.int32),
        pltpu.SMEM((cols, 1, slots), jnp.int32),
        pltpu.VMEM((fine_residual.shape[1] // edge,) + block, low),
        pltpu.VMEM((cols - 1, per_peer) + block, low),
        pltpu.VMEM((cols, per_peer) + block, low),
        pltpu.VMEM(tiles_one.shape, low),
        pltpu.VMEM(tiles_two.shape, low),
        pltpu.VMEM(tiles_three.shape, low),
        pltpu.VMEM((slots,) + block, wide),
        pltpu.VMEM((slots + 1,) + block, wide),
        pltpu.VMEM((tiles_two.shape[0] + 1,) + block, wide),
        pltpu.VMEM((tiles_three.shape[0] + 1,) + block, wide),
        pltpu.VMEM((rows, piece_one) + block, low),
        pltpu.VMEM((cols, piece_two) + block, low),
        pltpu.VMEM((rows, piece_three) + block, low),
        pltpu.VMEM((rows - 1, piece_one) + block, low),
        pltpu.VMEM((cols - 1, piece_two) + block, low),
        pltpu.VMEM((rows - 1, piece_three) + block, low),
        pltpu.VMEM((piece_one,) + block, wide),
        pltpu.VMEM((piece_two,) + block, wide),
        pltpu.VMEM((piece_three,) + block, wide),
        pltpu.VMEM((rows, piece_one) + block, low),
        pltpu.VMEM((cols, piece_two) + block, low),
        dma((7,)),
        dma((2, cols - 1)),
        dma((2, cols - 1)),
        dma((2, chunks, rows - 1)),
        dma((2, chunks, rows - 1)),
        dma((2, 1, cols - 1)),
        dma((2, 1, cols - 1)),
        dma((2, 1, rows - 1)),
    ]
    return pl.pallas_call(
        functools.partial(kernel, (rows, cols)),
        in_specs=[vmem] * 2 + [hbm] * 3 + [smem] * 5 + [vmem] * 3,
        out_specs=[vmem] * 3,
        out_shape=[
            jax.ShapeDtypeStruct((vectors, piece * edge), low) for piece in (piece_one, piece_two, piece_three)
        ],
        scratch_shapes=scratch,
        compiler_params=pltpu.CompilerParams(collective_id=0, has_side_effects=True),
        name="restrict_all",
    )(
        fine_residual,
        columns_one.reshape(1, slots),
        tiles_one,
        tiles_two,
        tiles_three,
        pointers_one,
        pointers_two,
        pointers_three,
        columns_two,
        columns_three,
        grouped(points_one),
        grouped(points_two),
        grouped(points_three),
    )


def solution(mesh):
    placed = (
        P(None, ("row", "col")),
        P(("row", "col"), None, None),
        P(("row", "col")),
        P(("row", "col")),
        P(("col", "row")),
        P(("row", "col"), None, None),
        P(("row", "col")),
        P(("row", "col")),
        P(("row", "col")),
        P(("row", "col"), None, None),
        P(("row", "col")),
        P(("row", "col")),
        P(("col", "row")),
    )
    return jax.shard_map(
        on_device,
        mesh=mesh,
        in_specs=placed,
        out_specs=(P(None, ("col", "row")), P(None, ("row", "col")), P(None, ("col", "row"))),
        check_vma=False,
    )
```

time: 113 us -> 71.7 us (0.63)
  Pallas kernels: 80.7 us -> 66.5 us
  starting transfers between devices: 8.76 us -> 0 us
  waiting for transfers between devices: 8.05 us -> 0 us
  other arithmetic: 5.69 us -> 0 us
  local copies, waits for them, and re-layouts: 8.38 us -> 4.24 us
    pallas_call x9 -> x1, Pallas kernels: 80.7 us -> 66.5 us  [on_device(): pl.pallas_call(functools.partial(kernel, (rows, cols)), in_specs=[vmem] *...]
    all_to_all x2 -> x0, starting transfers between devices: 8.76 us -> none  [the longest x1 5.2 us: on_device(): lax.all_to_all(requests, 'col', split_axis=0, concat_axis=0, tiled=True)]
    all_to_all x2 -> x0, waiting for transfers between devices: 8.05 us -> none  [the longest x1 4.5 us: on_device(): lax.all_to_all(requests, 'col', split_axis=0, concat_axis=0, tiled=True)]
    reshape x3 -> x0, local copies, waits for them, and re-layouts: 4.24 us -> none  [join_blocks(): jnp.transpose(blocks, (1, 0, 2))]
    unnamed x6 -> x3, local copies, waits for them, and re-layouts: 1 us -> 4.24 us
    reduce_sum x5 -> x0, other arithmetic: 2.64 us -> none  [the longest x3 2.35 us: segments(): jnp.sum((pointers[None, :] <= positions[:, None]).astype(jnp.int32), axis=1)]
    gather x1 -> x0, local copies, waits for them, and re-layouts: 1.77 us -> none  [on_device(): found = jnp.take(own_blocks, asked.reshape(-1), axis=0, mode='clip')]
    all_to_all x2 -> x0, local copies, waits for them, and re-layouts: 1.19 us -> none  [on_device(): lax.all_to_all(requests, 'col', split_axis=0, concat_axis=0, tiled=True)]
  transfers between devices with their start and end apart: 2 -> 0, of which waited for: 2 -> 0; matrix products, arithmetic and copies ran while one was open for 2% -> 0% of each run, Pallas kernels for 8% -> 0%
where the time goes in v1:
time: 71.7 us; the launch traced here: 71.4 us
  Pallas kernels  66.5 us (93%)
  local copies, waits for them, and re-layouts  4.24 us (6%)
    pallas_call x1, Pallas kernels, on_device(): pl.pallas_call(functools.partial(kernel, (rows, cols)), in_specs=[vmem] *...  66.5 us
    unnamed x3, local copies, waits for them, and re-layouts  4.24 us

profile of v1, /device:TPU:0, one launch (start us, length us, event | category | flops | bytes accessed | tf_op | source)
XLA Modules:
  0.0 71.4 jit_solution(3140959338038901921)
XLA Ops:
  0.6 66.5 %restrict_all.1 = (bf16[16,4096]{1,0:T(8,128)(2,1)}, bf16[16,1024]{1,0:T(8,128)(2,1)}, bf16[16,256]{1,0:T(8,128)(2,1)}) custom-call(bf16[16,16384]{1,0:T(8,128)(2,1)} %fine_ref.1, s32[1,256]{1,0:T(1,128)} %bitcast.6, bf16[256,128,128]{2,1,0:T(8,128)(2,1)} %tiles_one.1, bf16[128,128,128]{2,1,0:T(8,128)(2,1)} %tiles_two.1, bf16[16,128,128]{2,1,0:T(8,128)(2,1)} %tiles_three.1, ...), custom_call_target="tpu_custom_call" | custom-call | tf_op jit(solution)/shard_map/restrict_all/pallas_call | solution.py:484
  67.2 1.6 %copy.19 = bf16[16,4096]{1,0:T(8,128)(2,1)} copy(bf16[16,4096]{1,0:T(8,128)(2,1)} %get-tuple-element.6) | data formatting | bytes 262144
  68.7 1.4 %copy.20 = bf16[16,1024]{1,0:T(8,128)(2,1)} copy(bf16[16,1024]{1,0:T(8,128)(2,1)} %get-tuple-element.7) | data formatting | bytes 65536
  70.1 1.3 %copy.21 = bf16[16,256]{1,0:T(8,128)(2,1)} copy(bf16[16,256]{1,0:T(8,128)(2,1)} %get-tuple-element.8) | data formatting | bytes 16384

commit v2 on v1

v2 whole, which is shorter than its diff:
```python
import functools

import jax
import jax.numpy as jnp
from jax import lax
from jax.experimental import pallas as pl
from jax.experimental.pallas import tpu as pltpu
from jax.sharding import PartitionSpec as P

CHUNKS = 2
BATCH = 16


def mirrored(index, mask, count):
    flipped = index
    bit = 1
    while bit < count:
        if mask & bit:
            flipped = flipped + bit * (1 - 2 * lax.rem(index // bit, 2))
        bit *= 2
    return flipped


def mirror_order(count):
    return sorted(range(1, count), key=lambda mask: (bin(mask).count("1"), mask))


def shift_of(size):
    assert size & (size - 1) == 0
    return size.bit_length() - 1


def down(row):
    edge = 128
    parts = []
    for first in range(0, row.shape[1], edge):
        spread = jnp.broadcast_to(row[:, first : first + edge], (edge, edge))
        parts.append(jnp.transpose(spread, (1, 0)))
    return parts


def plan(columns_ref, live, peers, blocks_peer, requests_ref, slots_ref, targets_ref):
    slots = columns_ref.shape[1]
    edge = 128
    per_peer = slots // peers
    columns = columns_ref[...]
    places = lax.broadcasted_iota(jnp.int32, (1, slots), 1)
    owner = jnp.right_shift(columns, shift_of(blocks_peer))
    within = jnp.bitwise_and(columns, blocks_peer - 1)
    owner = jnp.where(places < live, owner, peers + places)
    rank = jnp.zeros((1, slots), jnp.int32)
    owners_down = down(owner)
    for part, other in enumerate(owners_down):
        lines = lax.broadcasted_iota(jnp.int32, (edge, edge), 0) + part * edge
        ranks = []
        for first in range(0, slots, edge):
            lanes = lax.broadcasted_iota(jnp.int32, (edge, edge), 1) + first
            here = jnp.broadcast_to(owner[:, first : first + edge], (edge, edge))
            same = jnp.where((other == here) & (lines < lanes), 1, 0)
            ranks.append(jnp.sum(same, axis=0, keepdims=True))
        rank = rank + jnp.concatenate(ranks, axis=1)
    target = jnp.where(places < live, owner * per_peer + rank, slots)
    targets_ref[...] = jnp.where(places < live, target, 0)
    targets_down = down(target)
    within_down = down(within)
    for first in range(0, slots, edge):
        lanes = lax.broadcasted_iota(jnp.int32, (edge, edge), 1) + first
        request = jnp.zeros((1, edge), jnp.int32)
        slot = jnp.zeros((1, edge), jnp.int32)
        for part in range(slots // edge):
            lines = lax.broadcasted_iota(jnp.int32, (edge, edge), 0) + part * edge
            hit = targets_down[part] == lanes
            request = request + jnp.sum(jnp.where(hit, within_down[part], 0), axis=0, keepdims=True)
            slot = slot + jnp.sum(jnp.where(hit, lines, 0), axis=0, keepdims=True)
        requests_ref[:, first : first + edge] = request
        slots_ref[:, first : first + edge] = slot


def pair_products(tiles, sources):
    none = jnp.zeros_like(sources[0])
    left = jnp.concatenate([sources[0], none], axis=1)
    right = jnp.concatenate([none, sources[1]], axis=1)
    both = lax.dot_general(
        jnp.concatenate([left, right], axis=0),
        jnp.concatenate(tiles, axis=1),
        (((1,), (1,)), ((), ())),
        preferred_element_type=jnp.float32,
    )
    vectors = sources[0].shape[0]
    return both[:vectors], both[vectors:]


def some_products(tiles_ref, number, tile_of, source_of):
    products = []
    for i in range(0, number, 2):
        products += pair_products(
            [tiles_ref[tile_of(i)], tiles_ref[tile_of(i + 1)]], [source_of(i), source_of(i + 1)]
        )
    return products


def points_groups(first, last, points_ref, block_of, blocks, span, out_ref):
    edge = out_ref.shape[2]
    vectors = out_ref.shape[1]
    wide = points_ref.shape[2]
    group = wide // edge

    def one_group(number, carry):
        points = points_ref[number]
        owners = jnp.broadcast_to(jnp.right_shift(points, shift_of(edge)), (vectors, wide))
        lanes = jnp.broadcast_to(jnp.bitwise_and(points, edge - 1), (edge, wide))
        spots = lax.broadcasted_iota(jnp.int32, (edge, wide), 0)
        pick = (lanes == spots).astype(jnp.float32).astype(jnp.bfloat16)
        found = jnp.zeros((vectors, wide), jnp.float32)
        for part in range(blocks // span):
            rows = jnp.concatenate([block_of(part * span + k) for k in range(span)], axis=0)
            moved = jnp.dot(rows, pick, preferred_element_type=jnp.float32)
            for k in range(span):
                here = moved[k * vectors : (k + 1) * vectors]
                found = jnp.where(owners == part * span + k, here, found)
        for i in range(group):
            out_ref[number * group + i] = found[:, i * edge : (i + 1) * edge]
        return carry

    lax.fori_loop(first, last, one_group, 0)


def kernel(axes, *refs):
    rows, cols = axes
    (fine_h, columns_h, pointers_one_h, pointers_two_h, pointers_three_h, columns_two_h, columns_three_h) = refs[:7]
    (points_one_h, points_two_h, points_three_h, tiles_one, tiles_two, tiles_three) = refs[7:13]
    out_one, out_two, out_three = refs[13:16]
    (fine_ref, columns_ref, pointers_one, pointers_two, pointers_three, columns_two, columns_three) = refs[16:23]
    (points_one, points_two, points_three, held_one, held_two, held_three) = refs[23:29]
    (requests_v, slots_v, targets_v, asked_v, slots_s, targets_s, asked_s) = refs[29:36]
    (fine_blocks, replies_out, replies, products_one, sums_one, sums_two, sums_three) = refs[36:43]
    (partial_one, partial_two, partial_three, arrived_one, passing, arrived_two, arrived_three) = refs[43:50]
    (injected_one, injected_two, injected_three, group_one, group_two) = refs[50:55]
    (load_sem, local_sem, request_sem, reply_sem, sum_one_sem, pass_sem, own_one_sem, on_sem) = refs[55:63]
    (sum_two_sem, own_two_sem, sum_three_sem) = refs[63:]

    row, col = lax.axis_index("row"), lax.axis_index("col")
    edge = held_one.shape[2]
    slots = columns_ref.shape[1]
    per_peer = slots // cols
    blocks_peer = fine_ref.shape[1] // edge
    row_peers = [(k, lax.rem(row + k, rows)) for k in range(1, rows)]
    col_peers = [(m, mirrored(col, m, cols)) for m in mirror_order(cols)]
    mesh_id = pl.DeviceIdType.MESH

    barrier = pltpu.get_barrier_semaphore()
    for _, peer in row_peers:
        pl.semaphore_signal(barrier, inc=1, device_id={"row": peer}, device_id_type=mesh_id)
    for _, peer in col_peers:
        pl.semaphore_signal(barrier, inc=1, device_id={"col": peer}, device_id_type=mesh_id)
    pairs = [
        (columns_h, columns_ref),
        (pointers_one_h, pointers_one),
        (fine_h, fine_ref),
        (points_one_h, points_one),
        (tiles_one, held_one),
        (pointers_two_h, pointers_two),
        (pointers_three_h, pointers_three),
        (columns_two_h, columns_two),
        (columns_three_h, columns_three),
        (points_two_h, points_two),
        (points_three_h, points_three),
        (tiles_two, held_two),
        (tiles_three, held_three),
    ]
    loads = [
        pltpu.make_async_copy(source, held, load_sem.at[i]) for i, (source, held) in enumerate(pairs)
    ]
    for load in loads:
        load.start()

    with jax.named_scope("wait_plan"):
        loads[0].wait()
        loads[1].wait()
    with jax.named_scope("plan"):
        plan(
            columns_ref,
            pointers_one[pointers_one.shape[0] - 1],
            cols,
            blocks_peer,
            requests_v,
            slots_v,
            targets_v,
        )
    plans = [
        pltpu.make_async_copy(requests_v, asked_s.at[0], local_sem.at[0]),
        pltpu.make_async_copy(slots_v, slots_s, local_sem.at[1]),
        pltpu.make_async_copy(targets_v, targets_s, local_sem.at[2]),
    ]
    with jax.named_scope("barrier"):
        pl.semaphore_wait(barrier, rows + cols - 2)

    def copy_to(source, target, out_sem, in_sem, device):
        return pltpu.make_async_remote_copy(
            src_ref=source,
            dst_ref=target,
            send_sem=out_sem,
            recv_sem=in_sem,
            device_id=device,
            device_id_type=mesh_id,
        )

    def send(source, target, sems, at, device):
        copy = copy_to(source, target, sems.at[(0,) + at], sems.at[(1,) + at], device)
        copy.start()
        return copy

    asks = [send(requests_v, asked_v.at[m - 1], request_sem, (m - 1,), {"col": peer}) for m, peer in col_peers]
    for copy in plans:
        copy.start()

    def take(m, out_ref, place):
        base = col * per_peer

        def some(step, carry):
            for i in range(8):
                at = step * 8 + i
                out_ref[place, at] = fine_blocks[asked_s[m, 0, base + at]]
            return carry

        lax.fori_loop(0, per_peer // 8, some, 0)

    def products_of(m, owner):
        base = owner * per_peer
        batch = min(BATCH, per_peer)

        def some(step, carry):
            first = step * batch
            found = some_products(
                held_one,
                batch,
                lambda i: slots_s[0, base + first + i],
                lambda i: replies[m, first + i],
            )
            for i, product in enumerate(found):
                products_one[base + first + i] = product
            return carry

        lax.fori_loop(0, per_peer // batch, some, 0)

    groups = points_one.shape[0]
    span_one = min(blocks_peer, 32)
    marks = [groups * part // 16 for part in (0, 5, 9, 13, 16)]

    def points_at_one(part):
        with jax.named_scope("points_one"):
            points_groups(
                marks[part],
                marks[part + 1],
                points_one,
                lambda j: fine_blocks[j],
                blocks_peer,
                span_one,
                injected_one,
            )

    with jax.named_scope("wait_fine"):
        loads[2].wait()
        loads[3].wait()
    with jax.named_scope("blocks"):
        for j in range(blocks_peer):
            fine_blocks[j] = fine_ref[:, j * edge : (j + 1) * edge]
    points_at_one(0)
    with jax.named_scope("wait_ask"):
        for copy in asks:
            copy.wait_recv()
        asked = pltpu.make_async_copy(asked_v, asked_s.at[pl.ds(1, cols - 1)], local_sem.at[3])
        asked.start()
        for copy in plans:
            copy.wait()
        take(0, replies, 0)
        asked.wait()
    answers = []
    with jax.named_scope("answer"):
        for m, peer in col_peers:
            take(m, replies_out, m - 1)
            answers.append(send(replies_out.at[m - 1], replies.at[m], reply_sem, (m - 1,), {"col": peer}))
    with jax.named_scope("wait_tiles"):
        loads[4].wait()
    products_of(0, col)
    points_at_one(1)
    for number, ((m, peer), copy) in enumerate(zip(col_peers, answers)):
        with jax.named_scope(f"wait_reply#m={m}"):
            copy.wait_recv()
        with jax.named_scope(f"products#m={m}"):
            products_of(m, peer)
        if number + 2 < len(marks) - 1:
            points_at_one(number + 2)
    for load in loads[5:]:
        load.wait()

    def run_one(step, total):
        for i in range(8):
            at = step * 8 + i
            total = total + products_one[targets_s[0, at]]
            sums_one[at + 1] = total
        return total

    with jax.named_scope("run_one"):
        sums_one[0] = jnp.zeros(sums_one.shape[1:], jnp.float32)
        lax.fori_loop(0, slots // 8, run_one, jnp.zeros(sums_one.shape[1:], jnp.float32))

    def block_sum(sums, pointers, block):
        return sums[pointers[block + 1]] - sums[pointers[block]]

    def partials(sums, pointers, partial, piece, first, size, more=None):
        per_piece = partial.shape[1]
        step_size = min(size, 8)

        def some(step, carry):
            for i in range(step_size):
                at = first + step * step_size + i
                total = block_sum(sums, pointers, piece * per_piece + at)
                if more is not None:
                    total = total + more[at].astype(jnp.float32)
                partial[piece, at] = total.astype(partial.dtype)
            return carry

        lax.fori_loop(0, size // step_size, some, 0)

    def along(first, last):
        for far in range(first, last, 1 if last > first else -1):
            for sign in (1, -1):
                other = row + sign * far
                yield far, sign, (other >= 0) & (other < rows), other

    end = rows - 1
    chunks = sum_one_sem.shape[1]
    size = partial_one.shape[1] // chunks
    parts = [pl.ds(h * size, size) for h in range(chunks)]
    waits = []

    def sum_copy(h, other):
        return copy_to(
            partial_one.at[other, parts[h]],
            arrived_one.at[row, parts[h]],
            sum_one_sem.at[0, h, other],
            sum_one_sem.at[1, h, row],
            {"row": other},
        )

    def sum_wait(h, other):
        return copy_to(
            partial_one.at[other, parts[h]],
            arrived_one.at[other, parts[h]],
            sum_one_sem.at[0, h, other],
            sum_one_sem.at[1, h, other],
            {"row": other},
        )

    def pass_copy(h, side, other, through):
        return copy_to(
            partial_one.at[other, parts[h]],
            passing.at[side, parts[h]],
            pass_sem.at[0, side, h],
            pass_sem.at[1, side, h],
            {"row": through},
        )

    sides = [(0, 0, 1, end), (1, end, end - 1, 0)]
    for h in range(chunks):
        with jax.named_scope(f"partials#h={h}"):
            for side, source, through, to in sides:

                @pl.when(row == source)
                def _():
                    partials(sums_one, pointers_one, partial_one, to, h * size, size)
                    pass_copy(h, side, to, through).start()

            for far, sign, valid, other in along(end - 1, 0):
                direct = valid
                if far == end - 1:
                    to = end if sign > 0 else 0
                    direct = valid & (other != to)

                @pl.when(direct)
                def _():
                    partials(sums_one, pointers_one, partial_one, other, h * size, size)
                    sum_copy(h, other).start()

    def pass_on(h):
        for side, source, through, to in sides:

            @pl.when(row == through)
            def _():
                pass_copy(h, side, to, through).wait_recv()
                partials(sums_one, pointers_one, partial_one, to, h * size, size, passing.at[side])
                sum_copy(h, to).start()

    def own_copy(h, piece, other, out_sem):
        return copy_to(
            group_one.at[piece, parts[h]],
            group_one.at[piece, parts[h]],
            out_sem,
            own_one_sem.at[1, h, piece],
            {"row": other},
        )

    def own_direct(far, other):
        if far == 1:
            return True
        return (other != 0) & (other != end)

    for h in range(chunks):
        with jax.named_scope(f"pass#h={h}"):
            pass_on(h)
        for far, sign, valid, other in along(1, rows):
            if far == end:
                continue

            @pl.when(valid)
            def _():
                with jax.named_scope(f"wait_sum#h={h}#far={far}"):
                    sum_wait(h, other).wait_recv()

        with jax.named_scope(f"own#h={h}"):
            base = row * partial_one.shape[1]

            def finish(i):
                at = h * size + i
                total = block_sum(sums_one, pointers_one, base + at) + injected_one[at]
                for other in range(rows):
                    comes = (row != other) & ((row - other) * (row - other) < end * end)
                    here = arrived_one[other, at].astype(jnp.float32)
                    total = total + jnp.where(comes, here, 0.0)
                value = total.astype(out_one.dtype)
                out_one[:, at * edge : (at + 1) * edge] = value
                group_one[row, at] = value

            for i in range(size):
                finish(i)
            for far, sign, valid, other in along(end, 0):

                @pl.when(valid & own_direct(far, other))
                def _():
                    own_copy(h, row, other, own_one_sem.at[0, h, other]).start()

    def points_at_two(first, last):
        with jax.named_scope("points_two"):
            points_groups(
                first,
                last,
                points_two,
                lambda j: group_one[row, j],
                group_one.shape[1],
                min(group_one.shape[1], 32),
                injected_two,
            )

    groups_two = points_two.shape[0]
    for h in range(chunks):
        for far in range(1, rows):
            for sign in (1, -1):
                other = row + sign * far
                valid = (other >= 0) & (other < rows)
                with jax.named_scope(f"wait_own#h={h}#far={far}"):

                    @pl.when(valid)
                    def _():
                        own_copy(h, other, row, own_one_sem.at[0, h, other]).wait_recv()

                    for to, through in ((end, end - 1), (0, 1)):

                        @pl.when(valid & (row == through) & ((other - to) * (other - to) > 1) & (other != to))
                        def _():
                            own_copy(h, other, to, on_sem.at[h, other]).start()

            if h == 0:
                points_at_two(groups_two * (far - 1) // end, groups_two * far // end)

    def drain_one():
        for h in range(chunks):
            for side, source, through, to in sides:

                @pl.when(row == source)
                def _():
                    pass_copy(h, side, to, through).wait_send()

                @pl.when(row == through)
                def _():
                    sum_copy(h, to).wait_send()

            for far, sign, valid, other in along(end - 1, 0):
                direct = valid
                if far == end - 1:
                    to = end if sign > 0 else 0
                    direct = valid & (other != to)

                @pl.when(direct)
                def _():
                    sum_copy(h, other).wait_send()

            for far, sign, valid, other in along(end, 0):

                @pl.when(valid & own_direct(far, other))
                def _():
                    own_copy(h, row, other, own_one_sem.at[0, h, other]).wait_send()

                for to, through in ((end, end - 1), (0, 1)):

                    @pl.when(valid & (row == through) & ((other - to) * (other - to) > 1) & (other != to))
                    def _():
                        own_copy(h, other, to, on_sem.at[h, other]).wait_send()

    def exchange(sums, pointers, partial, arrived, injected, peers, axis, me, sems, group, own_sems, out):
        size = partial.shape[1]
        first, again = [], []
        with jax.named_scope("partials"):
            for k, peer in peers:
                partials(sums, pointers, partial, peer, 0, size)
                first.append(send(partial.at[peer], arrived.at[k - 1], sems, (k - 1,), {axis: peer}))
        own = [block_sum(sums, pointers, me * size + i) + injected[i] for i in range(size)]
        for (k, _), copy in zip(peers, first):
            with jax.named_scope(f"wait_sum#k={k}"):
                copy.wait_recv()
            for i in range(size):
                own[i] = own[i] + arrived[k - 1, i].astype(jnp.float32)
        for i in range(size):
            value = own[i].astype(out.dtype)
            out[:, i * edge : (i + 1) * edge] = value
            if group is not None:
                group[me, i] = value
        if group is not None:
            for k, peer in peers:
                again.append(send(group.at[me], group.at[me], own_sems, (k - 1,), {axis: peer}))
        return first, again

    def restrict(held, columns, group, sums):
        number = held.shape[0]
        batch = min(2 * BATCH, number)
        per_piece = group.shape[1]

        def some(step, total):
            first = step * batch

            def source_of(i):
                column = columns[first + i]
                return group[jnp.right_shift(column, shift_of(per_piece)), jnp.bitwise_and(column, per_piece - 1)]

            found = some_products(held, batch, lambda i: first + i, source_of)
            for i, product in enumerate(found):
                total = total + product
                sums[first + i + 1] = total
            return total

        sums[0] = jnp.zeros(sums.shape[1:], jnp.float32)
        lax.fori_loop(0, number // batch, some, jnp.zeros(sums.shape[1:], jnp.float32))

    with jax.named_scope("restrict_two"):
        restrict(held_two, columns_two, group_one, sums_two)
    sent_two, own_two = exchange(
        sums_two, pointers_two, partial_two, arrived_two, injected_two, col_peers, "col", col, sum_two_sem, group_two,
        own_two_sem, out_two,
    )
    with jax.named_scope("points_three"):
        points_groups(
            0,
            points_three.shape[0],
            points_three,
            lambda j: group_two[col, j],
            group_two.shape[1],
            group_two.shape[1],
            injected_three,
        )
    with jax.named_scope("wait_group_two"):
        for copy in own_two:
            copy.wait_recv()
    with jax.named_scope("restrict_three"):
        restrict(held_three, columns_three, group_two, sums_three)
    sent_three, _ = exchange(
        sums_three, pointers_three, partial_three, arrived_three, injected_three, row_peers, "row", row, sum_three_sem,
        None, None, out_three,
    )
    with jax.named_scope("drain"):
        for copy in asks + answers + sent_two + own_two + sent_three:
            copy.wait_send()
        drain_one()


def tail_kernel(*refs):
    half = len(refs) // 2
    for source, out in zip(refs[:half], refs[half:]):
        out[...] = source[...]


def on_device(
    fine_residual,
    tiles_one,
    pointers_one,
    columns_one,
    points_one,
    tiles_two,
    pointers_two,
    columns_two,
    points_two,
    tiles_three,
    pointers_three,
    columns_three,
    points_three,
):
    vectors = fine_residual.shape[0]
    edge = tiles_one.shape[1]
    rows, cols = lax.axis_size("row"), lax.axis_size("col")
    slots = tiles_one.shape[0]
    per_peer = slots // cols
    low, wide = fine_residual.dtype, jnp.float32
    piece_one = (pointers_one.shape[0] - 1) // rows
    piece_two = (pointers_two.shape[0] - 1) // cols
    piece_three = (pointers_three.shape[0] - 1) // rows
    chunks = CHUNKS if piece_one % CHUNKS == 0 else 1

    def grouped(points):
        size = points.shape[0] // edge
        group = min(size, 2)
        return points.reshape(size // group, 1, group * edge)

    block = (vectors, edge)
    dma = pltpu.SemaphoreType.DMA
    inputs = [
        (fine_residual, pltpu.VMEM),
        (columns_one.reshape(1, slots), pltpu.VMEM),
        (pointers_one, pltpu.SMEM),
        (pointers_two, pltpu.SMEM),
        (pointers_three, pltpu.SMEM),
        (columns_two, pltpu.SMEM),
        (columns_three, pltpu.SMEM),
        (grouped(points_one), pltpu.VMEM),
        (grouped(points_two), pltpu.VMEM),
        (grouped(points_three), pltpu.VMEM),
        (tiles_one, pltpu.VMEM),
        (tiles_two, pltpu.VMEM),
        (tiles_three, pltpu.VMEM),
    ]
    scratch = [space(array.shape, array.dtype) for array, space in inputs]
    scratch += [
        pltpu.VMEM((1, slots), jnp.int32),
        pltpu.VMEM((1, slots), jnp.int32),
        pltpu.VMEM((1, slots), jnp.int32),
        pltpu.VMEM((cols - 1, 1, slots), jnp.int32),
        pltpu.SMEM((1, slots), jnp.int32),
        pltpu.SMEM((1, slots), jnp.int32),
        pltpu.SMEM((cols, 1, slots), jnp.int32),
        pltpu.VMEM((fine_residual.shape[1] // edge,) + block, low),
        pltpu.VMEM((cols - 1, per_peer) + block, low),
        pltpu.VMEM((cols, per_peer) + block, low),
        pltpu.VMEM((slots,) + block, wide),
        pltpu.VMEM((slots + 1,) + block, wide),
        pltpu.VMEM((tiles_two.shape[0] + 1,) + block, wide),
        pltpu.VMEM((tiles_three.shape[0] + 1,) + block, wide),
        pltpu.VMEM((rows, piece_one) + block, low),
        pltpu.VMEM((cols, piece_two) + block, low),
        pltpu.VMEM((rows, piece_three) + block, low),
        pltpu.VMEM((rows, piece_one) + block, low),
        pltpu.VMEM((2, piece_one) + block, low),
        pltpu.VMEM((cols - 1, piece_two) + block, low),
        pltpu.VMEM((rows - 1, piece_three) + block, low),
        pltpu.VMEM((piece_one,) + block, wide),
        pltpu.VMEM((piece_two,) + block, wide),
        pltpu.VMEM((piece_three,) + block, wide),
        pltpu.VMEM((rows, piece_one) + block, low),
        pltpu.VMEM((cols, piece_two) + block, low),
        dma((len(inputs),)),
        dma((4,)),
        dma((2, cols - 1)),
        dma((2, cols - 1)),
        dma((2, chunks, rows)),
        dma((2, 2, chunks)),
        dma((2, chunks, rows)),
        dma((chunks, rows)),
        dma((2, cols - 1)),
        dma((2, cols - 1)),
        dma((2, rows - 1)),
    ]
    shapes = [jax.ShapeDtypeStruct((vectors, piece * edge), low) for piece in (piece_one, piece_two, piece_three)]
    vmem = [pl.BlockSpec(memory_space=pltpu.VMEM)] * 3
    found = pl.pallas_call(
        functools.partial(kernel, (rows, cols)),
        in_specs=[pl.BlockSpec(memory_space=pl.ANY)] * len(inputs),
        out_specs=vmem,
        out_shape=shapes,
        scratch_shapes=scratch,
        compiler_params=pltpu.CompilerParams(
            collective_id=0, has_side_effects=True
        ),
        name="restrict_all",
    )(*[array for array, _ in inputs])
    return pl.pallas_call(
        tail_kernel,
        in_specs=vmem,
        out_specs=vmem,
        out_shape=shapes,
        name="results",
    )(*found)


def solution(mesh):
    placed = (
        P(None, ("row", "col")),
        P(("row", "col"), None, None),
        P(("row", "col")),
        P(("row", "col")),
        P(("col", "row")),
        P(("row", "col"), None, None),
        P(("row", "col")),
        P(("row", "col")),
        P(("row", "col")),
        P(("row", "col"), None, None),
        P(("row", "col")),
        P(("row", "col")),
        P(("col", "row")),
    )
    return jax.shard_map(
        on_device,
        mesh=mesh,
        in_specs=placed,
        out_specs=(P(None, ("col", "row")), P(None, ("row", "col")), P(None, ("col", "row"))),
        check_vma=False,
    )
```

time: 71.7 us -> 66.6 us (0.929)
  local copies, waits for them, and re-layouts: 4.24 us -> 0 us
    unnamed x3 -> x0, local copies, waits for them, and re-layouts: 4.24 us -> none
    pallas_call x1 -> x2, Pallas kernels: 66.5 us -> 65.8 us  [the longest x1 64.2 us: on_device(): pl.pallas_call(functools.partial(kernel, (rows, cols)), in_specs=[pl.Bloc...]
where the time goes in v2:
time: 66.6 us; the launch traced here: 66.4 us
  Pallas kernels  65.8 us (99%)
    pallas_call x1, Pallas kernels, on_device(): pl.pallas_call(functools.partial(kernel, (rows, cols)), in_specs=[pl.Bloc...  64.2 us
    pallas_call x1, Pallas kernels, on_device(): pl.pallas_call(tail_kernel, in_specs=vmem, out_specs=vmem, out_shape=shap...  1.6 us

profile of v2, /device:TPU:0, one launch (start us, length us, event | category | flops | bytes accessed | tf_op | source)
XLA Modules:
  0.0 66.4 jit_solution(15233325521438256956)
XLA Ops:
  0.6 64.2 %restrict_all.1 = (bf16[16,4096]{1,0:T(8,128)(2,1)}, bf16[16,1024]{1,0:T(8,128)(2,1)}, bf16[16,256]{1,0:T(8,128)(2,1)}) custom-call(bf16[16,16384]{1,0:T(8,128)(2,1)} %refs_0_.1, s32[1,256]{1,0:T(1,128)} %bitcast.6, s32[129]{0:T(256)} %refs_2_.1, s32[65]{0:T(128)} %refs_3_.1, s32[9]{0:T(128)} %refs_4_.1, s32[128]{0:T(128)} %refs_5_.1, s32[16]{0:T(128)} %refs_6_.1, ...), custom_call_target="tpu_custom_call" | custom-call | tf_op jit(solution)/shard_map/restrict_all/pallas_call | solution.py:681
  64.8 1.6 %results.1 = (bf16[16,4096]{1,0:T(8,128)(2,1)}, bf16[16,1024]{1,0:T(8,128)(2,1)}, bf16[16,256]{1,0:T(8,128)(2,1)}) custom-call(bf16[16,4096]{1,0:T(8,128)(2,1)} %get-tuple-element.6.refs_0_, bf16[16,1024]{1,0:T(8,128)(2,1)} %get-tuple-element.7.refs_1_, bf16[16,256]{1,0:T(8,128)(2,1)} %get-tuple-element.8.refs_2_), custom_call_target="tpu_custom_call" | custom-call | tf_op jit(solution)/shard_map/results/pallas_call | solution.py:692

commit v3 on v2

--- a/solution.py
+++ b/solution.py
@@ -7,7 +7,7 @@
 from jax.experimental.pallas import tpu as pltpu
 from jax.sharding import PartitionSpec as P
 
-CHUNKS = 2
+SPLIT = (1, 1, 1, 1)
 BATCH = 16
 
 
@@ -23,6 +23,10 @@
 
 def mirror_order(count):
     return sorted(range(1, count), key=lambda mask: (bin(mask).count("1"), mask))
+
+
+def far_order(count):
+    return sorted(range(1, count), key=lambda mask: (-bin(mask >> 1).count("1"), mask & 1, mask))
 
 
 def shift_of(size):
@@ -132,12 +136,12 @@
     out_one, out_two, out_three = refs[13:16]
     (fine_ref, columns_ref, pointers_one, pointers_two, pointers_three, columns_two, columns_three) = refs[16:23]
     (points_one, points_two, points_three, held_one, held_two, held_three) = refs[23:29]
-    (requests_v, slots_v, targets_v, asked_v, slots_s, targets_s, asked_s) = refs[29:36]
-    (fine_blocks, replies_out, replies, products_one, sums_one, sums_two, sums_three) = refs[36:43]
-    (partial_one, partial_two, partial_three, arrived_one, passing, arrived_two, arrived_three) = refs[43:50]
-    (injected_one, injected_two, injected_three, group_one, group_two) = refs[50:55]
-    (load_sem, local_sem, request_sem, reply_sem, sum_one_sem, pass_sem, own_one_sem, on_sem) = refs[55:63]
-    (sum_two_sem, own_two_sem, sum_three_sem) = refs[63:]
+    (requests_v, slots_v, targets_v, slots_s, targets_s, asked_s) = refs[29:35]
+    (fine_blocks, replies_out, replies, products_one, sums_one, sums_two, sums_three) = refs[35:42]
+    (partial_one, partial_two, partial_three, arrived_one, passing, arrived_two, arrived_three) = refs[42:49]
+    (injected_one, injected_two, injected_three, group_one, group_two) = refs[49:54]
+    (load_sem, local_sem, request_sem, reply_sem, sum_one_sem, pass_sem, own_one_sem, on_sem) = refs[54:62]
+    (sum_two_sem, own_two_sem, sum_three_sem) = refs[62:]
 
     row, col = lax.axis_index("row"), lax.axis_index("col")
     edge = held_one.shape[2]
@@ -146,6 +150,7 @@
     blocks_peer = fine_ref.shape[1] // edge
     row_peers = [(k, lax.rem(row + k, rows)) for k in range(1, rows)]
     col_peers = [(m, mirrored(col, m, cols)) for m in mirror_order(cols)]
+    far_peers = [(m, mirrored(col, m, cols)) for m in far_order(cols)]
     mesh_id = pl.DeviceIdType.MESH
 
     barrier = pltpu.get_barrier_semaphore()
@@ -210,7 +215,7 @@
         copy.start()
         return copy
 
-    asks = [send(requests_v, asked_v.at[m - 1], request_sem, (m - 1,), {"col": peer}) for m, peer in col_peers]
+    asks = [send(requests_v, asked_s.at[m], request_sem, (m - 1,), {"col": peer}) for m, peer in col_peers]
     for copy in plans:
         copy.start()
 
@@ -269,12 +274,9 @@
     with jax.named_scope("wait_ask"):
         for copy in asks:
             copy.wait_recv()
-        asked = pltpu.make_async_copy(asked_v, asked_s.at[pl.ds(1, cols - 1)], local_sem.at[3])
-        asked.start()
         for copy in plans:
             copy.wait()
         take(0, replies, 0)
-        asked.wait()
     answers = []
     with jax.named_scope("answer"):
         for m, peer in col_peers:
@@ -284,7 +286,8 @@
         loads[4].wait()
     products_of(0, col)
     points_at_one(1)
-    for number, ((m, peer), copy) in enumerate(zip(col_peers, answers)):
+    coming = list(zip(col_peers, answers))
+    for number, ((m, peer), copy) in enumerate(coming):
         with jax.named_scope(f"wait_reply#m={m}"):
             copy.wait_recv()
         with jax.named_scope(f"products#m={m}"):
@@ -331,9 +334,10 @@
 
     end = rows - 1
     chunks = sum_one_sem.shape[1]
-    size = partial_one.shape[1] // chunks
-    parts = [pl.ds(h * size, size) for h in range(chunks)]
-    waits = []
+    share = partial_one.shape[1] // sum(SPLIT)
+    starts = [sum(SPLIT[:h]) * share for h in range(chunks)]
+    sizes = [part * share for part in SPLIT]
+    parts = [pl.ds(start, size) for start, size in zip(starts, sizes)]
 
     def sum_copy(h, other):
         return copy_to(
@@ -369,7 +373,7 @@
 
                 @pl.when(row == source)
                 def _():
-                    partials(sums_one, pointers_one, partial_one, to, h * size, size)
+                    partials(sums_one, pointers_one, partial_one, to, starts[h], sizes[h])
                     pass_copy(h, side, to, through).start()
 
             for far, sign, valid, other in along(end - 1, 0):
@@ -380,7 +384,7 @@
 
                 @pl.when(direct)
                 def _():
-                    partials(sums_one, pointers_one, partial_one, other, h * size, size)
+                    partials(sums_one, pointers_one, partial_one, other, starts[h], sizes[h])
                     sum_copy(h, other).start()
 
     def pass_on(h):
@@ -389,7 +393,7 @@
             @pl.when(row == through)
             def _():
                 pass_copy(h, side, to, through).wait_recv()
-                partials(sums_one, pointers_one, partial_one, to, h * size, size, passing.at[side])
+                partials(sums_one, pointers_one, partial_one, to, starts[h], sizes[h], passing.at[side])
                 sum_copy(h, to).start()
 
     def own_copy(h, piece, other, out_sem):
@@ -422,7 +426,7 @@
             base = row * partial_one.shape[1]
 
             def finish(i):
-                at = h * size + i
+                at = starts[h] + i
                 total = block_sum(sums_one, pointers_one, base + at) + injected_one[at]
                 for other in range(rows):
                     comes = (row != other) & ((row - other) * (row - other) < end * end)
@@ -432,7 +436,7 @@
                 out_one[:, at * edge : (at + 1) * edge] = value
                 group_one[row, at] = value
 
-            for i in range(size):
+            for i in range(sizes[h]):
                 finish(i)
             for far, sign, valid, other in along(end, 0):
 
@@ -554,7 +558,7 @@
     with jax.named_scope("restrict_two"):
         restrict(held_two, columns_two, group_one, sums_two)
     sent_two, own_two = exchange(
-        sums_two, pointers_two, partial_two, arrived_two, injected_two, col_peers, "col", col, sum_two_sem, group_two,
+        sums_two, pointers_two, partial_two, arrived_two, injected_two, far_peers, "col", col, sum_two_sem, group_two,
         own_two_sem, out_two,
     )
     with jax.named_scope("points_three"):
@@ -612,7 +616,7 @@
     piece_one = (pointers_one.shape[0] - 1) // rows
     piece_two = (pointers_two.shape[0] - 1) // cols
     piece_three = (pointers_three.shape[0] - 1) // rows
-    chunks = CHUNKS if piece_one % CHUNKS == 0 else 1
+    chunks = len(SPLIT)
 
     def grouped(points):
         size = points.shape[0] // edge
@@ -641,7 +645,6 @@
         pltpu.VMEM((1, slots), jnp.int32),
         pltpu.VMEM((1, slots), jnp.int32),
         pltpu.VMEM((1, slots), jnp.int32),
-        pltpu.VMEM((cols - 1, 1, slots), jnp.int32),
         pltpu.SMEM((1, slots), jnp.int32),
         pltpu.SMEM((1, slots), jnp.int32),
         pltpu.SMEM((cols, 1, slots), jnp.int32),
@@ -665,7 +668,7 @@
         pltpu.VMEM((rows, piece_one) + block, low),
         pltpu.VMEM((cols, piece_two) + block, low),
         dma((len(inputs),)),
-        dma((4,)),
+        dma((3,)),
         dma((2, cols - 1)),
         dma((2, cols - 1)),
         dma((2, chunks, rows)),

time: 66.6 us -> 63.9 us (0.959)
  Pallas kernels: 65.8 us -> 63.1 us
    pallas_call x1, Pallas kernels: 64.2 us -> 61.5 us  [on_device(): pl.pallas_call(functools.partial(kernel, (rows, cols)), in_specs=[pl.Bloc...]
where the time goes in v3:
time: 63.9 us; the launch traced here: 63.7 us
  Pallas kernels  63.1 us (99%)
  between operations  0.64 us (1%)
    pallas_call x1, Pallas kernels, on_device(): pl.pallas_call(functools.partial(kernel, (rows, cols)), in_specs=[pl.Bloc...  61.5 us
    pallas_call x1, Pallas kernels, on_device(): pl.pallas_call(tail_kernel, in_specs=vmem, out_specs=vmem, out_shape=shap...  1.6 us

profile of v3, /device:TPU:0, one launch (start us, length us, event | category | flops | bytes accessed | tf_op | source)
XLA Modules:
  0.0 63.7 jit_solution(12726183732274014623)
XLA Ops:
  0.6 61.5 %restrict_all.1 = (bf16[16,4096]{1,0:T(8,128)(2,1)}, bf16[16,1024]{1,0:T(8,128)(2,1)}, bf16[16,256]{1,0:T(8,128)(2,1)}) custom-call(bf16[16,16384]{1,0:T(8,128)(2,1)} %refs_0_.1, s32[1,256]{1,0:T(1,128)} %bitcast.6, s32[129]{0:T(256)} %refs_2_.1, s32[65]{0:T(128)} %refs_3_.1, s32[9]{0:T(128)} %refs_4_.1, s32[128]{0:T(128)} %refs_5_.1, s32[16]{0:T(128)} %refs_6_.1, ...), custom_call_target="tpu_custom_call" | custom-call | tf_op jit(solution)/shard_map/restrict_all/pallas_call | solution.py:684
  62.1 1.6 %results.1 = (bf16[16,4096]{1,0:T(8,128)(2,1)}, bf16[16,1024]{1,0:T(8,128)(2,1)}, bf16[16,256]{1,0:T(8,128)(2,1)}) custom-call(bf16[16,4096]{1,0:T(8,128)(2,1)} %get-tuple-element.6.refs_0_, bf16[16,1024]{1,0:T(8,128)(2,1)} %get-tuple-element.7.refs_1_, bf16[16,256]{1,0:T(8,128)(2,1)} %get-tuple-element.8.refs_2_), custom_call_target="tpu_custom_call" | custom-call | tf_op jit(solution)/shard_map/results/pallas_call | solution.py:695

commit v4 on v3

--- a/solution.py
+++ b/solution.py
@@ -9,6 +9,8 @@
 
 SPLIT = (1, 1, 1, 1)
 BATCH = 16
+LEAD = 0
+STRAIGHT = 1
 
 
 def mirrored(index, mask, count):
@@ -367,25 +369,32 @@
         )
 
     sides = [(0, 0, 1, end), (1, end, end - 1, 0)]
-    for h in range(chunks):
+    def send_ends(h):
+        for side, source, through, to in sides:
+
+            @pl.when(row == source)
+            def _():
+                partials(sums_one, pointers_one, partial_one, to, starts[h], sizes[h])
+                pass_copy(h, side, to, through).start()
+
+    def send_sums(h):
+        for far, sign, valid, other in along(end - 1, 0):
+            direct = valid
+            if far == end - 1:
+                to = end if sign > 0 else 0
+                direct = valid & (other != to)
+
+            @pl.when(direct)
+            def _():
+                partials(sums_one, pointers_one, partial_one, other, starts[h], sizes[h])
+                sum_copy(h, other).start()
+
+    for h in range(chunks + LEAD):
         with jax.named_scope(f"partials#h={h}"):
-            for side, source, through, to in sides:
-
-                @pl.when(row == source)
-                def _():
-                    partials(sums_one, pointers_one, partial_one, to, starts[h], sizes[h])
-                    pass_copy(h, side, to, through).start()
-
-            for far, sign, valid, other in along(end - 1, 0):
-                direct = valid
-                if far == end - 1:
-                    to = end if sign > 0 else 0
-                    direct = valid & (other != to)
-
-                @pl.when(direct)
-                def _():
-                    partials(sums_one, pointers_one, partial_one, other, starts[h], sizes[h])
-                    sum_copy(h, other).start()
+            if h < chunks:
+                send_ends(h)
+            if h >= LEAD:
+                send_sums(h - LEAD)
 
     def pass_on(h):
         for side, source, through, to in sides:
@@ -405,12 +414,15 @@
             {"row": other},
         )
 
-    def own_direct(far, other):
-        if far == 1:
+    def straight(h):
+        return h >= chunks - STRAIGHT
+
+    def own_direct(h, far, other):
+        if far == 1 or (far == end and straight(h)):
             return True
         return (other != 0) & (other != end)
 
-    for h in range(chunks):
+    def sum_up(h):
         with jax.named_scope(f"pass#h={h}"):
             pass_on(h)
         for far, sign, valid, other in along(1, rows):
@@ -440,7 +452,7 @@
                 finish(i)
             for far, sign, valid, other in along(end, 0):
 
-                @pl.when(valid & own_direct(far, other))
+                @pl.when(valid & own_direct(h, far, other))
                 def _():
                     own_copy(h, row, other, own_one_sem.at[0, h, other]).start()
 
@@ -456,6 +468,41 @@
                 injected_two,
             )
 
+    def onwards(h, valid, other):
+        for to, through in ((end, end - 1), (0, 1)):
+            gap = (other - to) * (other - to)
+            onward = valid & (row == through) & (gap > 1)
+            if straight(h):
+                onward = onward & (gap < end * end)
+            yield to, onward
+
+    def early(h, valid, other):
+        passed = False
+        for _, onward in onwards(h, valid, other):
+            passed = passed | onward
+        return passed & (other != 0) & (other != end)
+
+    def receive(h, other, wanted):
+        @pl.when(wanted)
+        def _():
+            own_copy(h, other, row, own_one_sem.at[0, h, other]).wait_recv()
+
+        for to, onward in onwards(h, wanted, other):
+
+            @pl.when(onward)
+            def _():
+                own_copy(h, other, to, on_sem.at[h, other]).start()
+
+    def receive_early(h):
+        for far, sign, valid, other in along(1, rows):
+            receive(h, other, early(h, valid, other))
+
+    for h in range(chunks):
+        sum_up(h)
+        if h > 0:
+            receive_early(h - 1)
+    receive_early(chunks - 1)
+
     groups_two = points_two.shape[0]
     for h in range(chunks):
         for far in range(1, rows):
@@ -463,17 +510,7 @@
                 other = row + sign * far
                 valid = (other >= 0) & (other < rows)
                 with jax.named_scope(f"wait_own#h={h}#far={far}"):
-
-                    @pl.when(valid)
-                    def _():
-                        own_copy(h, other, row, own_one_sem.at[0, h, other]).wait_recv()
-
-                    for to, through in ((end, end - 1), (0, 1)):
-
-                        @pl.when(valid & (row == through) & ((other - to) * (other - to) > 1) & (other != to))
-                        def _():
-                            own_copy(h, other, to, on_sem.at[h, other]).start()
-
+                    receive(h, other, valid & jnp.logical_not(early(h, valid, other)))
             if h == 0:
                 points_at_two(groups_two * (far - 1) // end, groups_two * far // end)
 
@@ -501,13 +538,13 @@
 
             for far, sign, valid, other in along(end, 0):
 
-                @pl.when(valid & own_direct(far, other))
+                @pl.when(valid & own_direct(h, far, other))
                 def _():
                     own_copy(h, row, other, own_one_sem.at[0, h, other]).wait_send()
 
-                for to, through in ((end, end - 1), (0, 1)):
-
-                    @pl.when(valid & (row == through) & ((other - to) * (other - to) > 1) & (other != to))
+                for to, onward in onwards(h, valid, other):
+
+                    @pl.when(onward)
                     def _():
                         own_copy(h, other, to, on_sem.at[h, other]).wait_send()
 

time: 63.9 us -> 62.2 us (0.973)
  Pallas kernels: 63.1 us -> 61.4 us
    pallas_call x1, Pallas kernels: 61.5 us -> 59.8 us  [on_device(): pl.pallas_call(functools.partial(kernel, (rows, cols)), in_specs=[pl.Bloc...]
where the time goes in v4:
time: 62.2 us; the launch traced here: 62 us
  Pallas kernels  61.4 us (99%)
  between operations  0.64 us (1%)
    pallas_call x1, Pallas kernels, on_device(): pl.pallas_call(functools.partial(kernel, (rows, cols)), in_specs=[pl.Bloc...  59.8 us
    pallas_call x1, Pallas kernels, on_device(): pl.pallas_call(tail_kernel, in_specs=vmem, out_specs=vmem, out_shape=shap...  1.6 us

profile of v4, /device:TPU:0, one launch (start us, length us, event | category | flops | bytes accessed | tf_op | source)
XLA Modules:
  0.0 62.0 jit_solution(8494556585133154059)
XLA Ops:
  0.6 59.8 %restrict_all.1 = (bf16[16,4096]{1,0:T(8,128)(2,1)}, bf16[16,1024]{1,0:T(8,128)(2,1)}, bf16[16,256]{1,0:T(8,128)(2,1)}) custom-call(bf16[16,16384]{1,0:T(8,128)(2,1)} %refs_0_.1, s32[1,256]{1,0:T(1,128)} %bitcast.6, s32[129]{0:T(256)} %refs_2_.1, s32[65]{0:T(128)} %refs_3_.1, s32[9]{0:T(128)} %refs_4_.1, s32[128]{0:T(128)} %refs_5_.1, s32[16]{0:T(128)} %refs_6_.1, ...), custom_call_target="tpu_custom_call" | custom-call | tf_op jit(solution)/shard_map/restrict_all/pallas_call | solution.py:721
  60.4 1.6 %results.1 = (bf16[16,4096]{1,0:T(8,128)(2,1)}, bf16[16,1024]{1,0:T(8,128)(2,1)}, bf16[16,256]{1,0:T(8,128)(2,1)}) custom-call(bf16[16,4096]{1,0:T(8,128)(2,1)} %get-tuple-element.6.refs_0_, bf16[16,1024]{1,0:T(8,128)(2,1)} %get-tuple-element.7.refs_1_, bf16[16,256]{1,0:T(8,128)(2,1)} %get-tuple-element.8.refs_2_), custom_call_target="tpu_custom_call" | custom-call | tf_op jit(solution)/shard_map/results/pallas_call | solution.py:732

commit v5 on v4

--- a/solution.py
+++ b/solution.py
@@ -276,14 +276,14 @@
     with jax.named_scope("wait_ask"):
         for copy in asks:
             copy.wait_recv()
-        for copy in plans:
-            copy.wait()
-        take(0, replies, 0)
     answers = []
     with jax.named_scope("answer"):
         for m, peer in col_peers:
             take(m, replies_out, m - 1)
             answers.append(send(replies_out.at[m - 1], replies.at[m], reply_sem, (m - 1,), {"col": peer}))
+    for copy in plans:
+        copy.wait()
+    take(0, replies, 0)
     with jax.named_scope("wait_tiles"):
         loads[4].wait()
     products_of(0, col)
@@ -573,7 +573,7 @@
 
     def restrict(held, columns, group, sums):
         number = held.shape[0]
-        batch = min(2 * BATCH, number)
+        batch = min(4 * BATCH, number)
         per_piece = group.shape[1]
 
         def some(step, total):

time: 62.2 us -> 61.9 us (level)
  no operation moved by 1% of the time
where the time goes in v5:
time: 61.9 us; the launch traced here: 61.7 us
  Pallas kernels  61.1 us (99%)
  between operations  0.64 us (1%)
    pallas_call x1, Pallas kernels, on_device(): pl.pallas_call(functools.partial(kernel, (rows, cols)), in_specs=[pl.Bloc...  59.5 us
    pallas_call x1, Pallas kernels, on_device(): pl.pallas_call(tail_kernel, in_specs=vmem, out_specs=vmem, out_shape=shap...  1.6 us

profile of v5, /device:TPU:0, one launch (start us, length us, event | category | flops | bytes accessed | tf_op | source)
XLA Modules:
  0.0 61.7 jit_solution(8307285423395970586)
XLA Ops:
  0.6 59.5 %restrict_all.1 = (bf16[16,4096]{1,0:T(8,128)(2,1)}, bf16[16,1024]{1,0:T(8,128)(2,1)}, bf16[16,256]{1,0:T(8,128)(2,1)}) custom-call(bf16[16,16384]{1,0:T(8,128)(2,1)} %refs_0_.1, s32[1,256]{1,0:T(1,128)} %bitcast.6, s32[129]{0:T(256)} %refs_2_.1, s32[65]{0:T(128)} %refs_3_.1, s32[9]{0:T(128)} %refs_4_.1, s32[128]{0:T(128)} %refs_5_.1, s32[16]{0:T(128)} %refs_6_.1, ...), custom_call_target="tpu_custom_call" | custom-call | tf_op jit(solution)/shard_map/restrict_all/pallas_call | solution.py:721
  60.1 1.6 %results.1 = (bf16[16,4096]{1,0:T(8,128)(2,1)}, bf16[16,1024]{1,0:T(8,128)(2,1)}, bf16[16,256]{1,0:T(8,128)(2,1)}) custom-call(bf16[16,4096]{1,0:T(8,128)(2,1)} %get-tuple-element.6.refs_0_, bf16[16,1024]{1,0:T(8,128)(2,1)} %get-tuple-element.7.refs_1_, bf16[16,256]{1,0:T(8,128)(2,1)} %get-tuple-element.8.refs_2_), custom_call_target="tpu_custom_call" | custom-call | tf_op jit(solution)/shard_map/results/pallas_call | solution.py:732
